TPU v7x, 32 devices: a whole 2x2x4 slice. The times are simulated.
32 devices in a mesh: dp: 8 (over y, x, core), tensor: 4 (over z).
Axes of the slice: x: 2, y: 2, z: 4, core: 2. Of those that a mesh axis runs over, the one named last changes fastest.
Arguments:
- grad_tokens: bfloat16 [1536, 2048], P('dp', 'tensor'), may hold values from -6 to 6
- hidden_input: bfloat16 [2048, 5120], P('dp', 'tensor'), may hold values from -6 to 6
- output_weight: bfloat16 [5120, 2048], P(None, 'tensor'), may hold values from -0.078125 to 0.078125
- image_tokens: int32 [8, 8], replicated, may hold values from 0 to 192, as said below
- moved_images: int32 [8], replicated, may hold values from 0 to 7, as said below
Outputs:
- input_grad: bfloat16 [2048, 5120], P('dp', 'tensor')
- weight_grad: float32 [5120, 2048], P('dp', 'tensor')
- bias_grad: float32 [2048], P('tensor')
Inputs may be any that keep to these rules, and one draw needn't show every extreme that they name: `image_tokens`: row s lists the merged tokens of sample s's images in order: 1 to 8 positive entries, then zeros; each row sums to 192. `moved_images`: entry s is less than the number of images of sample s; those trailing images hold at most 64 merged tokens together, exactly 64 for some sample in every draw. They are encoded by owner s + 1 (owner 0 after the last).
All inputs are finite; a program needn't handle non-finite values.
Results may differ from a plain program's by a relative error of at most 0.014.
Values may be sent and summed in bfloat16 or wider, within the bound.
A program may use at most 64 MiB of HBM per device.

v0:
```python
import jax
import jax.numpy as jnp
from jax import lax
from jax.sharding import PartitionSpec as P

root_half = 0.7071067811865476
inv_root_tau = 0.3989422804014327


def from_behind(value, axis, steps):
    count = lax.axis_size(axis)
    pairs = [(source, (source + steps) % count) for source in range(count)]
    return lax.ppermute(value, axis, pairs)


def gelu_parts(values):
    normal_cdf = 0.5 * (1.0 + jax.scipy.special.erf(values * root_half))
    density = jnp.exp(-0.5 * values * values) * inv_root_tau
    return (values * normal_cdf, normal_cdf + values * density)


def kept_lengths(image_tokens, moved_images):
    present = jnp.sum((image_tokens > 0).astype(jnp.int32), axis=1)
    slot_ids = jnp.arange(image_tokens.shape[1], dtype=jnp.int32)
    kept_mask = slot_ids[None, :] < (present - moved_images)[:, None]
    return jnp.sum(jnp.where(kept_mask, image_tokens, 0), axis=1)


def per_device(grad_tokens, hidden_input, output_weight, image_tokens, moved_images):
    dp_count = lax.axis_size("dp")
    dp_index = lax.axis_index("dp")
    tok_rows = grad_tokens.shape[0]
    buffer_rows = hidden_input.shape[0]
    tail_count = buffer_rows - tok_rows
    keep_len = kept_lengths(image_tokens, moved_images)
    own_keep = jnp.sum(jnp.where(jnp.arange(dp_count, dtype=jnp.int32) == dp_index, keep_len, 0))
    positions = jnp.arange(tok_rows, dtype=jnp.int32)[:, None]
    zero_value = jnp.zeros((), jnp.bfloat16)
    kept_rows = jnp.where(positions < own_keep, grad_tokens, zero_value)
    moving = jnp.where(
        positions[tok_rows - tail_count :] >= own_keep,
        grad_tokens[tok_rows - tail_count :],
        zero_value,
    )
    arrived = from_behind(moving, "dp", 1)
    grad_rows = jnp.concatenate([kept_rows, arrived], axis=0)
    bias_grad = lax.psum(jnp.sum(grad_tokens.astype(jnp.float32), axis=0), "dp")
    activation, slopes = gelu_parts(hidden_input.astype(jnp.float32))
    partials = lax.dot_general(
        grad_rows, output_weight, (((1,), (1,)), ((), ())), preferred_element_type=jnp.float32
    )
    grad_hidden = lax.psum_scatter(
        partials.astype(jnp.bfloat16), "tensor", scatter_dimension=1, tiled=True
    ).astype(jnp.float32)
    input_grad = (grad_hidden * slopes).astype(jnp.bfloat16)
    gathered_input = lax.all_gather(hidden_input, "tensor", axis=1, tiled=True)
    full_act = gelu_parts(gathered_input.astype(jnp.float32))[0].astype(jnp.bfloat16)
    hidden_width = full_act.shape[1]
    rows_each = (hidden_width + 8 * dp_count - 1) // (8 * dp_count) * 8
    padded = jnp.pad(full_act, ((0, 0), (0, rows_each * dp_count - hidden_width)))
    weight_grad = lax.psum_scatter(
        lax.dot_general(
            padded, grad_rows, (((0,), (0,)), ((), ())), preferred_element_type=jnp.float32
        ),
        "dp",
        scatter_dimension=0,
        tiled=True,
    )
    return (input_grad, weight_grad, bias_grad)


def solution(mesh):
    return jax.shard_map(
        per_device,
        mesh=mesh,
        in_specs=(P("dp", "tensor"), P("dp", "tensor"), P(None, "tensor"), P(), P()),
        out_specs=(P("dp", "tensor"), P("dp", "tensor"), P("tensor")),
        check_vma=False,
    )
```

profile of v0, /device:TPU:0, one launch (start us, length us, event | category | flops | bytes accessed | tf_op | source)
XLA Modules:
  0.0 212.5 jit_solution(6390169746239598268)
XLA Ops:
  7.2 0.0 all-gather.2.cloned.1.call-start
  7.2 0.7 all-gather.2.cloned.1.call-update
  7.9 0.0 reduce-scatter.3.cloned.1.call-start
  7.9 0.8 convert_reduce_fusion.1
  8.8 0.7 sub.3
  9.4 0.9 select_reduce_fusion
  10.3 0.6 fusion.17
  10.9 0.7 compare_bitcast_fusion
  11.6 0.9 slice_select_fusion
  12.5 0.5 collective-permute-start
  13.0 0.6 iota_compare_fusion.1
  13.7 1.0 broadcast_select_fusion
  14.7 3.1 %collective-permute-done = bf16[64,512]{1,0:T(8,128)(2,1)S(1)} collective-permute-done((bf16[64,512]{1,0:T(8,128)(2,1)S(1)}, bf16[64,512]{1,0:T(8,128)(2,1)S(1)}, u32[]{:S(2)}, u32[]{:S(2)}) %collective-permute-start) | collective-permute-done | bytes 65568 | tf_op jit(solution)/shard_map/ppermute | solution.py:13
  17.9 5.9 %convolution_convert_fusion = bf16[256,5120]{1,0:T(8,128)(2,1)} fusion(bf16[5120,512]{1,0:T(8,128)(2,1)} %param.7, bf16[64,512]{1,0:T(8,128)(2,1)S(1)} %collective-permute-done, bf16[192,512]{1,0:T(8,128)(2,1)S(1)} %broadcast_select_fusion), kind=kOutput, calls=%fused_computation.2 | convolution fusion | flops 1344012288 | bytes 8126464 | tf_op jit(solution)/shard_map/dot_general | solution.py:49
  23.8 0.0 reduce-scatter.3.cloned.1.call-update
  23.8 0.0 reduce-scatter.5.cloned.1.call-start
  23.8 43.2 %all-gather.2.cloned.1.call-done = bf16[256,5120]{1,0:T(8,128)(2,1)} async-done(((bf16[256,1280]{1,0:T(8,128)(2,1)}), bf16[256,5120]{1,0:T(8,128)(2,1)}) %all-gather.2.cloned.1.call-update) | async-done | bytes 2621456 | tf_op jit(solution)/shard_map/all_gather | solution.py:56
  67.0 7.3 %fusion.4 = f32[5120,512]{1,0:T(8,128)} fusion(bf16[256,5120]{1,0:T(8,128)(2,1)} %all-gather.2.cloned.1.call-done, bf16[64,512]{1,0:T(8,128)(2,1)S(1)} %collective-permute-done, bf16[192,512]{1,0:T(8,128)(2,1)S(1)} %broadcast_select_fusion), kind=kOutput, calls=%fused_computation.7 | convolution fusion | flops 1350565888 | bytes 13369344 | tf_op jit(solution)/shard_map/dot_general | solution.py:62
  74.4 0.0 reduce-scatter.5.cloned.1.call-update
  74.4 0.9 copy-done.1
  75.3 14.6 %psum.7 = f32[512]{0:T(512)} all-reduce(f32[512]{0:T(512)S(1)} %convert_reduce_fusion), channel_id=1, replica_groups=mesh['dp'=8,'tensor'=4] {'dp'}, use_global_device_ids=true, to_apply=%region_6.7 | all-reduce | flops 512 | bytes 4096 | tf_op jit(solution)/shard_map/psum | solution.py:47
  89.9 30.5 %reduce-scatter.3.cloned.1.call-done = bf16[256,1280]{1,0:T(8,128)(2,1)} async-done(((bf16[256,5120]{1,0:T(8,128)(2,1)}), bf16[256,1280]{1,0:T(8,128)(2,1)}) %reduce-scatter.3.cloned.1.call-update) | async-done | bytes 655376 | tf_op jit(solution)/shard_map/reduce_scatter | solution.py:52
  120.4 2.5 %fusion.16 = bf16[256,1280]{1,0:T(8,128)(2,1)} fusion(bf16[256,1280]{1,0:T(8,128)(2,1)S(1)} %copy-done, bf16[256,1280]{1,0:T(8,128)(2,1)} %reduce-scatter.3.cloned.1.call-done), kind=kLoop, calls=%fused_computation.22 | loop fusion | flops 3932160 | bytes 1966080 | tf_op jit(solution)/shard_map/convert_element_type | solution.py:55
  122.9 83.1 %reduce-scatter.5.cloned.1.call-done = f32[640,512]{1,0:T(8,128)} async-done(((f32[5120,512]{1,0:T(8,128)}), f32[640,512]{1,0:T(8,128)}) %reduce-scatter.5.cloned.1.call-update) | async-done | bytes 1310736 | tf_op jit(solution)/shard_map/reduce_scatter | solution.py:61
  (4 shorter events, 0.1 us)
Async XLA Ops:
  7.2 59.9 %all-gather.2.cloned.1.call-start = ((), (), s32[]{:S(2)}) async-start(), calls=%async_computation.3 | async-start | bytes 3276800 | tf_op jit(solution)/shard_map/all_gather | solution.py:56
  7.9 112.5 %reduce-scatter.3.cloned.1.call-start = ((), (), s32[]{:S(2)}) async-start(), calls=%async_computation.2 | async-start | bytes 3276800 | tf_op jit(solution)/shard_map/reduce_scatter | solution.py:52
  12.5 5.4 %collective-permute-start = (bf16[64,512]{1,0:T(8,128)(2,1)S(1)}, bf16[64,512]{1,0:T(8,128)(2,1)S(1)}, u32[]{:S(2)}, u32[]{:S(2)}) collective-permute-start(bf16[64,512]{1,0:T(8,128)(2,1)S(1)} %slice_select_fusion), channel_id=1, source_target_pairs={{0,4},{4,8},{8,12},{12,16},{16,20},{20,24},{24,28},{28,0},{1,5},{5... | collective-permute-start | bytes 196616 | tf_op jit(solution)/shard_map/ppermute | solution.py:13
  23.8 182.2 %reduce-scatter.5.cloned.1.call-start = ((), (), s32[]{:S(2)}) async-start(), calls=%async_computation.4 | async-start | bytes 11796480 | tf_op jit(solution)/shard_map/reduce_scatter | solution.py:61
  74.4 0.9 copy-start.1
  74.4 46.0 %copy-start = (bf16[256,1280]{1,0:T(8,128)(2,1)S(1)}, bf16[256,1280]{1,0:T(8,128)(2,1)}, u32[]{:S(2)}) copy-start(bf16[256,1280]{1,0:T(8,128)(2,1)} %param.6) | copy-start | bytes 1966084
Sparse Core Ops, SparseCore 0:
  9.5 57.4 all-gather.1
  69.3 51.0 reduce-scatter.2
  124.5 81.4 reduce-scatter.4
where the time goes:
time: 213 us
  waiting for transfers between devices  161 us (76%)
  blocking collectives  14.6 us (7%)
  between operations  13.8 us (6%)
  matrix products  13.2 us (6%)
  other arithmetic  8.8 us (4%)
    reduce_scatter x1, waiting for transfers between devices, per_device(): lax.psum_scatter(lax.dot_general(padded, grad_rows, (((0,), (0,)), ((), (...  83.1 us
    all_gather x1, waiting for transfers between devices, per_device(): gathered_input = lax.all_gather(hidden_input, 'tensor', axis=1, tiled=True)  43.2 us
    reduce_scatter x1, waiting for transfers between devices, per_device(): lax.psum_scatter(partials.astype(jnp.bfloat16), 'tensor', scatter_dimensi...  30.5 us
    psum x1, blocking collectives, per_device(): bias_grad = lax.psum(jnp.sum(grad_tokens.astype(jnp.float32), axis=0), 'dp')  14.6 us
    dot_general x1, matrix products, per_device(): lax.dot_general(padded, grad_rows, (((0,), (0,)), ((), ())), preferred_el...  7.31 us
    dot_general x1, matrix products, per_device(): lax.dot_general(grad_rows, output_weight, (((1,), (1,)), ((), ())), prefe...  5.9 us
  transfers between devices with their start and end apart: 4, of which 4 were waited for; matrix products, arithmetic and copies ran while one was open for 10% of the time, Pallas kernels for 0%

commit v1 on v0

v1 whole, which is shorter than its diff:
```python
import functools

import jax
import jax.numpy as jnp
from jax import lax
from jax.experimental import pallas as pl
from jax.experimental.pallas import tpu as pltpu
from jax.sharding import PartitionSpec as P

root_half = 0.7071067811865476
inv_root_tau = 0.3989422804014327
MESH = pl.DeviceIdType.MESH
F32 = jnp.float32
BF16 = jnp.bfloat16


def from_behind(value, axis, steps):
    count = lax.axis_size(axis)
    pairs = [(source, (source + steps) % count) for source in range(count)]
    return lax.ppermute(value, axis, pairs)


def gelu_parts(values):
    normal_cdf = 0.5 * (1.0 + lax.erf(values * root_half))
    density = jnp.exp(-0.5 * values * values) * inv_root_tau
    return (values * normal_cdf, normal_cdf + values * density)


def kept_lengths(image_tokens, moved_images):
    present = jnp.sum((image_tokens > 0).astype(jnp.int32), axis=1)
    slot_ids = jnp.arange(image_tokens.shape[1], dtype=jnp.int32)
    kept_mask = slot_ids[None, :] < (present - moved_images)[:, None]
    return jnp.sum(jnp.where(kept_mask, image_tokens, 0), axis=1)


def per_device_any(grad_tokens, hidden_input, output_weight, image_tokens, moved_images):
    dp_count = lax.axis_size("dp")
    dp_index = lax.axis_index("dp")
    tok_rows = grad_tokens.shape[0]
    buffer_rows = hidden_input.shape[0]
    tail_count = buffer_rows - tok_rows
    keep_len = kept_lengths(image_tokens, moved_images)
    own_keep = jnp.sum(jnp.where(jnp.arange(dp_count, dtype=jnp.int32) == dp_index, keep_len, 0))
    positions = jnp.arange(tok_rows, dtype=jnp.int32)[:, None]
    zero_value = jnp.zeros((), BF16)
    kept_rows = jnp.where(positions < own_keep, grad_tokens, zero_value)
    moving = jnp.where(
        positions[tok_rows - tail_count :] >= own_keep,
        grad_tokens[tok_rows - tail_count :],
        zero_value,
    )
    arrived = from_behind(moving, "dp", 1)
    grad_rows = jnp.concatenate([kept_rows, arrived], axis=0)
    bias_grad = lax.psum(jnp.sum(grad_tokens.astype(F32), axis=0), "dp")
    activation, slopes = gelu_parts(hidden_input.astype(F32))
    partials = lax.dot_general(
        grad_rows, output_weight, (((1,), (1,)), ((), ())), preferred_element_type=F32
    )
    grad_hidden = lax.psum_scatter(
        partials.astype(BF16), "tensor", scatter_dimension=1, tiled=True
    ).astype(F32)
    input_grad = (grad_hidden * slopes).astype(BF16)
    full_act = lax.all_gather(activation.astype(BF16), "tensor", axis=1, tiled=True)
    hidden_width = full_act.shape[1]
    rows_each = (hidden_width + 8 * dp_count - 1) // (8 * dp_count) * 8
    padded = jnp.pad(full_act, ((0, 0), (0, rows_each * dp_count - hidden_width)))
    weight_grad = lax.psum_scatter(
        lax.dot_general(
            padded, grad_rows, (((0,), (0,)), ((), ())), preferred_element_type=F32
        ),
        "dp",
        scatter_dimension=0,
        tiled=True,
    )
    return (input_grad, weight_grad, bias_grad)


def kernel(
    n, dpn,
    g_ref, x_ref, w_hbm, it_ref, mv_ref,
    xg_ref, wg_ref, bg_ref,
    w_ref, raw, tail, act, act_other, slope, grad, part, sbuf, up_in, dn_in, wsend, wrecv, wmid, bias,
    w_sem, core_s, core_r, act_s, act_r, tail_s, tail_r,
    up_s, up_r, dn_s, dn_r, pl_s, pl_r, mid_r, bi_s, bi_r,
):
    dp = lax.axis_index("dp")
    z = lax.axis_index("tensor")
    core = lax.rem(dp, 2)
    chip = lax.div(dp, 2)
    partner = dp + 1 - 2 * core
    chips = dpn // 2
    tok = g_ref.shape[0]
    rows = x_ref.shape[0]
    width = x_ref.shape[1]
    half = width // 2
    tails = rows - tok

    wcopy = pltpu.make_async_copy(w_hbm, w_ref, w_sem)
    wcopy.start()

    barrier = pltpu.get_barrier_semaphore()
    for k in range(1, dpn):
        pl.semaphore_signal(barrier, inc=1, device_id=(lax.rem(dp + k, dpn), z), device_id_type=MESH)

    @pl.when(z > 0)
    def _():
        pl.semaphore_signal(barrier, inc=1, device_id=(dp, z - 1), device_id_type=MESH)

    @pl.when(z < n - 1)
    def _():
        pl.semaphore_signal(barrier, inc=1, device_id=(dp, z + 1), device_id_type=MESH)

    pl.semaphore_wait(barrier, dpn - 1 + jnp.where(z > 0, 1, 0) + jnp.where(z < n - 1, 1, 0))

    def remote(src, dst, ss, rs, d, t):
        return pltpu.make_async_remote_copy(
            src_ref=src, dst_ref=dst, send_sem=ss, recv_sem=rs, device_id=(d, t), device_id_type=MESH
        )

    lane = 128
    nk = half // lane
    ptile = width // nk

    raw_copy = remote(g_ref, raw, core_s, core_r, partner, z)
    tail_src = g_ref.at[pl.ds(tok - tails, tails)]
    tail_copies = [
        remote(tail_src, tail, tail_s.at[k], tail_r, lax.rem(dp + 1 + k, dpn), z) for k in range(2)
    ]

    def act_copy(k):
        return remote(act_other.at[k], act.at[z, k, core], act_s.at[k], act_r.at[k], partner, z)

    step_rows = 64

    def gelu_tile(which, k, to_other):
        cols = pl.ds(pl.multiple_of(which * half + k * lane, lane), lane)

        def body(i, carry):
            rs = pl.ds(pl.multiple_of(i * step_rows, step_rows), step_rows)
            a, s = gelu_parts(x_ref[rs, cols].astype(F32))
            slope[rs, cols] = s
            if to_other:
                act_other[k, rs, :] = a.astype(BF16)
            else:
                act[z, k, core, rs, :] = a.astype(BF16)
            return carry

        lax.fori_loop(0, rows // step_rows, body, 0)

    def up_ag(h, k, r):
        return remote(act.at[h, k], act.at[h, k], up_s.at[r, k], up_r.at[r, k], dp, z + 1)

    def dn_ag(h, k, r):
        return remote(act.at[h, k], act.at[h, k], dn_s.at[r, k], dn_r.at[r, k], dp, z - 1)

    def up_rs(h, k, r):
        return remote(sbuf.at[h, k], up_in.at[h, k], up_s.at[r, k], up_r.at[r, k], dp, z + 1)

    def dn_rs(h, k, r):
        return remote(sbuf.at[h, k], dn_in.at[h, k], dn_s.at[r, k], dn_r.at[r, k], dp, z - 1)

    def send_own(k):
        act_copy(k).wait_recv()

        @pl.when(z < n - 1)
        def _():
            up_ag(z, k, 0).start()

        @pl.when(z > 0)
        def _():
            dn_ag(z, k, 0).start()

    for k in range(nk):
        gelu_tile(1 - core, k, True)
        act_copy(k).start()
        if k == 0:
            raw_copy.start()

            @pl.when(core == 1)
            def _():
                for c in tail_copies:
                    c.start()

        gelu_tile(core, k, False)
        if k > 0:
            send_own(k - 1)
    send_own(nk - 1)

    raw_copy.wait_recv()
    chip_sum = jnp.sum(g_ref[...].astype(F32), axis=0, keepdims=True) + jnp.sum(
        raw[...].astype(F32), axis=0, keepdims=True
    )
    bias[chip] = jnp.broadcast_to(chip_sum, bias.shape[1:])

    def keep_of(s):
        images = it_ref[pl.ds(s, 1), :].astype(F32)
        present = jnp.sum(jnp.where(images > 0, 1.0, 0.0), axis=1, keepdims=True)
        ids = lax.broadcasted_iota(jnp.int32, images.shape, 1).astype(F32)
        kept = jnp.where(ids < present - mv_ref[s].astype(F32), images, 0.0)
        return jnp.sum(kept, axis=1, keepdims=True)

    place = lax.broadcasted_iota(jnp.int32, (tok, g_ref.shape[1]), 0).astype(F32)
    zero = jnp.zeros((), F32)

    def masked_own(block, s):
        return jnp.where(place < keep_of(s), block.astype(F32), zero).astype(BF16)

    def masked_tail(block, s):
        return jnp.where(place[tok - tails :] >= keep_of(s), block.astype(F32), zero).astype(BF16)

    grad[core, 0:tok, :] = masked_own(g_ref[...], dp)
    grad[1 - core, 0:tok, :] = masked_own(raw[...], partner)
    first = 2 * chip

    @pl.when(core == 0)
    def _():
        grad[1, tok:rows, :] = masked_tail(g_ref[pl.ds(tok - tails, tails), :], first)

    @pl.when(core == 1)
    def _():
        grad[1, tok:rows, :] = masked_tail(raw[pl.ds(tok - tails, tails), :], first)

    tail_copies[0].wait_recv()
    grad[0, tok:rows, :] = masked_tail(tail[...], lax.rem(first + dpn - 1, dpn))

    def bias_copy(k):
        return remote(
            bias.at[chip], bias.at[chip], bi_s.at[k], bi_r.at[chip], lax.rem(dp + 2 * k, dpn), z
        )

    for k in range(1, chips):
        bias_copy(k).start()

    wcopy.wait()

    def all_h(i, carry):
        h = lax.div(i, nk)
        k = lax.rem(i, nk)
        at = pl.ds(pl.multiple_of(i * ptile, ptile), ptile)
        part[h, k] = lax.dot_general(
            grad[core], w_ref[at, :], (((1,), (1,)), ((), ())), preferred_element_type=F32
        )
        return carry

    lax.fori_loop(0, n * nk, all_h, 0)

    @pl.when(z == 0)
    def _():
        for r in range(1, n):
            for k in range(nk):
                sbuf[n - r, k] = part[n - r, k].astype(BF16)
                up_rs(n - r, k, r).start()

    @pl.when(z == n - 1)
    def _():
        for r in range(1, n):
            for k in range(nk):
                sbuf[r - 1, k] = part[r - 1, k].astype(BF16)
                dn_rs(r - 1, k, r).start()

    piece = lane // 2

    def relation(h):
        return jnp.where(lax.rem(chip, 2) != lax.rem(h, 2), 1, 0) + jnp.where(
            lax.div(chip, 2) != lax.div(h, 2), 2, 0
        )

    along_x = chip + 1 - 2 * lax.rem(chip, 2)
    along_y = lax.rem(chip + 2, chips)

    def owner_copy(h, k, j):
        role = relation(h) - 1
        return remote(
            wsend.at[h, k, j], wrecv.at[role, k, j], pl_s.at[h, k, j], pl_r.at[role, k, j], h * 2 + core, z
        )

    def corner_copy(h, k, j):
        through = along_x if j == 0 else along_y
        return remote(
            wsend.at[h, k, j], wmid.at[1 - j, k], pl_s.at[h, k, j], mid_r.at[1 - j, k], through * 2 + core, z
        )

    def merge(h, k):
        rel = relation(h)
        for role in (1, 2):
            late = 1 if role == 1 else 0

            @pl.when(rel == role)
            def _():
                corner_copy(h, k, late).wait_recv()
                wsend[h, k, late] = (
                    wsend[h, k, late].astype(F32) + wmid[role - 1, k].astype(F32)
                ).astype(BF16)
                owner_copy(h, k, late).start()

    def weight_tile(h, k):
        acc = lax.dot_general(
            act[h, k, 0], grad[0], (((0,), (0,)), ((), ())), preferred_element_type=F32
        ) + lax.dot_general(
            act[h, k, 1], grad[1], (((0,), (0,)), ((), ())), preferred_element_type=F32
        )
        rel = relation(h)

        @pl.when(rel == 0)
        def _():
            wg_ref[k * lane : (k + 1) * lane, :] = acc

        @pl.when(rel != 0)
        def _():
            for j in range(2):
                wsend[h, k, j] = acc[j * piece : (j + 1) * piece].astype(BF16)

        @pl.when(rel == 1)
        def _():
            owner_copy(h, k, 0).start()

        @pl.when(rel == 2)
        def _():
            owner_copy(h, k, 1).start()

        @pl.when(rel == 3)
        def _():
            for j in range(2):
                corner_copy(h, k, j).start()

    for k in range(nk):
        weight_tile(z, k)

    def merge_round(r, k):
        if r == 0:
            merge(z, k)
        else:

            @pl.when(z >= r)
            def _():
                merge(z - r, k)

            @pl.when(z + r <= n - 1)
            def _():
                merge(z + r, k)

    for r in range(1, n):
        for k in range(nk):

            @pl.when(z >= r)
            def _():
                up_ag(z - r, k, r - 1).wait_recv()

                @pl.when(z < n - 1)
                def _():
                    up_ag(z - r, k, r).start()

            @pl.when(z + r <= n - 1)
            def _():
                dn_ag(z + r, k, r - 1).wait_recv()

                @pl.when(z > 0)
                def _():
                    dn_ag(z + r, k, r).start()

            @pl.when((z > 0) & (z < r))
            def _():
                h = n + z - r
                up_rs(h, k, r - 1).wait_recv()
                sbuf[h, k] = (part[h, k] + up_in[h, k].astype(F32)).astype(BF16)
                up_rs(h, k, r).start()

            @pl.when((z < n - 1) & (z + r > n - 1))
            def _():
                h = z + r - n
                dn_rs(h, k, r - 1).wait_recv()
                sbuf[h, k] = (part[h, k] + dn_in[h, k].astype(F32)).astype(BF16)
                dn_rs(h, k, r).start()

            @pl.when(z >= r)
            def _():
                weight_tile(z - r, k)

            @pl.when(z + r <= n - 1)
            def _():
                weight_tile(z + r, k)

            merge_round(r - 1, k)
            if r == n - 1 and k >= 2:
                merge_round(r, k - 2)
    for k in range(max(nk - 2, 0), nk):
        merge_round(n - 1, k)

    for k in range(1, chips):
        source = lax.rem(chip + k, chips)
        remote(
            bias.at[source], bias.at[source], bi_s.at[k], bi_r.at[source], lax.rem(dp + 2 * k, dpn), z
        ).wait_recv()
    total = bias[0]
    for k in range(1, chips):
        total = total + bias[k]
    bg_ref[...] = total[0]

    for k in range(nk):
        for j in range(2):
            rs = slice(k * lane + j * piece, k * lane + (j + 1) * piece)
            acc = wg_ref[rs, :]
            for role in range(2):
                remote(
                    wsend.at[along_x, k, j], wrecv.at[role, k, j], pl_s.at[0, k, j], pl_r.at[role, k, j],
                    partner, z,
                ).wait_recv()
                acc = acc + wrecv[role, k, j].astype(F32)
            wg_ref[rs, :] = acc

    for k in range(nk):

        @pl.when(z > 0)
        def _():
            up_rs(z, k, n - 1).wait_recv()
            part[z, k] += up_in[z, k].astype(F32)

        @pl.when(z < n - 1)
        def _():
            dn_rs(z, k, n - 1).wait_recv()
            part[z, k] += dn_in[z, k].astype(F32)

        at = slice(k * ptile, (k + 1) * ptile)
        xg_ref[:, at] = (part[z, k] * slope[:, at]).astype(BF16)

    raw_copy.wait_send()

    @pl.when(core == 1)
    def _():
        for c in tail_copies:
            c.wait_send()

    for c in range(1, chips):
        bias_copy(c).wait_send()
        h = lax.rem(chip + c, chips)
        for k in range(nk):
            for j in range(2):
                remote(
                    wsend.at[h, k, j], wrecv.at[0, k, j], pl_s.at[h, k, j], pl_r.at[0, k, j], partner, z
                ).wait_send()
    for k in range(nk):
        act_copy(k).wait_send()
        for r in range(n):

            @pl.when(z < n - 1)
            def _():
                up_rs(0, k, r).wait_send()

            @pl.when(z > 0)
            def _():
                dn_rs(0, k, r).wait_send()


def per_device_fast(n, dpn, grad_tokens, hidden_input, output_weight, image_tokens, moved_images):
    tok, cols = grad_tokens.shape
    rows, width = hidden_input.shape
    half = width // 2
    chips = dpn // 2
    lane = 128
    nk = half // lane
    ptile = width // nk
    dma = pltpu.SemaphoreType.DMA
    vmem = pl.BlockSpec(memory_space=pltpu.VMEM)
    return pl.pallas_call(
        functools.partial(kernel, n, dpn),
        out_shape=(
            jax.ShapeDtypeStruct((rows, width), BF16),
            jax.ShapeDtypeStruct((half, cols), F32),
            jax.ShapeDtypeStruct((cols,), F32),
        ),
        in_specs=[
            vmem, vmem, pl.BlockSpec(memory_space=pl.ANY), vmem, pl.BlockSpec(memory_space=pltpu.SMEM),
        ],
        out_specs=(vmem, vmem, vmem),
        scratch_shapes=[
            pltpu.VMEM(output_weight.shape, BF16),
            pltpu.VMEM((tok, cols), BF16),
            pltpu.VMEM((rows - tok, cols), BF16),
            pltpu.VMEM((n, nk, 2, rows, lane), BF16),
            pltpu.VMEM((nk, rows, lane), BF16),
            pltpu.VMEM((rows, width), F32),
            pltpu.VMEM((2, rows, cols), BF16),
            pltpu.VMEM((n, nk, rows, ptile), F32),
            pltpu.VMEM((n, nk, rows, ptile), BF16),
            pltpu.VMEM((n, nk, rows, ptile), BF16),
            pltpu.VMEM((n, nk, rows, ptile), BF16),
            pltpu.VMEM((chips, nk, 2, lane // 2, cols), BF16),
            pltpu.VMEM((2, nk, 2, lane // 2, cols), BF16),
            pltpu.VMEM((2, nk, lane // 2, cols), BF16),
            pltpu.VMEM((chips, 8, cols), F32),
            dma,
            dma,
            dma,
            dma((nk,)),
            dma((nk,)),
            dma((2,)),
            dma,
            dma((n, nk)),
            dma((n, nk)),
            dma((n, nk)),
            dma((n, nk)),
            dma((chips, nk, 2)),
            dma((2, nk, 2)),
            dma((2, nk)),
            dma((chips,)),
            dma((chips,)),
        ],
        compiler_params=pltpu.CompilerParams(
            collective_id=0, has_side_effects=True, vmem_limit_bytes=60 * 1024 * 1024
        ),
    )(grad_tokens, hidden_input, output_weight, image_tokens, moved_images)


def solution(mesh):
    n, dpn = mesh.shape["tensor"], mesh.shape["dp"]
    fast = dpn == 2 * n == 2 * 2 * 2
    return jax.shard_map(
        functools.partial(per_device_fast, n, dpn) if fast else per_device_any,
        mesh=mesh,
        in_specs=(P("dp", "tensor"), P("dp", "tensor"), P(None, "tensor"), P(), P()),
        out_specs=(P("dp", "tensor"), P("dp", "tensor"), P("tensor")),
        check_vma=False,
    )
```

time: 213 us -> 72.6 us (0.34)
  waiting for transfers between devices: 161 us -> 0 us
  Pallas kernels: 0 us -> 68.1 us
  blocking collectives: 14.6 us -> 0 us
  matrix products: 13.2 us -> 0 us
  between operations: 13.8 us -> 0.65 us
  other arithmetic: 8.8 us -> 0 us
  local copies, waits for them, and re-layouts: 0.91 us -> 3.71 us
    reduce_scatter x2 -> x0, waiting for transfers between devices: 114 us -> none  [the longest x1 83.1 us: per_device(): lax.psum_scatter(lax.dot_general(padded, grad_rows, (((0,), (0,)), ((), (...]
    pallas_call x0 -> x1, Pallas kernels: none -> 68.1 us  [per_device_fast(): pl.pallas_call(functools.partial(kernel, n, dpn), out_shape=(jax.ShapeDty...]
    all_gather x1 -> x0, waiting for transfers between devices: 43.2 us -> none  [per_device(): gathered_input = lax.all_gather(hidden_input, 'tensor', axis=1, tiled=True)]
    psum x1 -> x0, blocking collectives: 14.6 us -> none  [per_device(): bias_grad = lax.psum(jnp.sum(grad_tokens.astype(jnp.float32), axis=0), 'dp')]
    dot_general x2 -> x0, matrix products: 13.2 us -> none  [the longest x1 7.31 us: per_device(): lax.dot_general(padded, grad_rows, (((0,), (0,)), ((), ())), preferred_el...]
    ppermute x1 -> x0, waiting for transfers between devices: 3.13 us -> none  [from_behind(): return lax.ppermute(value, axis, pairs)]
    unnamed x4 -> x7, local copies, waits for them, and re-layouts: 0.91 us -> 3.71 us
    convert_element_type x1 -> x0, other arithmetic: 2.54 us -> none  [per_device(): input_grad = (grad_hidden * slopes).astype(jnp.bfloat16)]
  transfers between devices with their start and end apart: 4 -> 0, of which waited for: 4 -> 0; matrix products, arithmetic and copies ran while one was open for 10% -> 0% of each run, Pallas kernels for 0% -> 0%
where the time goes in v1:
time: 72.6 us; the launch traced here: 72.4 us
  Pallas kernels  68.1 us (94%)
  local copies, waits for them, and re-layouts  3.71 us (5%)
    pallas_call x1, Pallas kernels, per_device_fast(): pl.pallas_call(functools.partial(kernel, n, dpn), out_shape=(jax.ShapeDty...  68.1 us
    unnamed x7, local copies, waits for them, and re-layouts  3.71 us

profile of v1, /device:TPU:0, one launch (start us, length us, event | category | flops | bytes accessed | tf_op | source)
XLA Modules:
  0.0 72.4 jit_solution(8034197879788422284)
XLA Ops:
  0.6 68.1 %shard_map.76 = (bf16[256,1280]{1,0:T(8,128)(2,1)}, f32[640,512]{1,0:T(8,128)}, f32[512]{0:T(512)}) custom-call(bf16[192,512]{1,0:T(8,128)(2,1)} %g_ref.1, bf16[256,1280]{1,0:T(8,128)(2,1)} %x_ref.1, bf16[5120,512]{1,0:T(8,128)(2,1)} %w_hbm.1, s32[8,8]{1,0:T(8,128)} %it_ref.1, s32[8]{0:T(128)} %mv_ref.1), custom_call_target="tpu_custom_call" | custom-call | tf_op jit(solution)/shard_map/pallas_call | solution.py:464
  68.7 0.0 copy-start
  68.7 2.1 %copy.11 = bf16[256,1280]{1,0:T(8,128)(2,1)} copy(bf16[256,1280]{1,0:T(8,128)(2,1)} %get-tuple-element.6) | data formatting | bytes 1310720
  70.8 0.0 copy-done
  70.8 0.0 copy-start.1
  70.8 1.1 %copy.12 = f32[640,512]{1,0:T(8,128)} copy(f32[640,512]{1,0:T(8,128)S(1)} %copy-done) | data formatting | bytes 2621440
  71.8 0.0 copy-done.1
  71.8 0.6 copy.13
Async XLA Ops:
  68.7 2.1 %copy-start = (f32[640,512]{1,0:T(8,128)S(1)}, f32[640,512]{1,0:T(8,128)}, u32[]{:S(2)}) copy-start(f32[640,512]{1,0:T(8,128)} %get-tuple-element.7) | copy-start | bytes 3932164
  70.8 1.1 %copy-start.1 = (f32[512]{0:T(512)S(1)}, f32[512]{0:T(512)}, u32[]{:S(2)}) copy-start(f32[512]{0:T(512)} %get-tuple-element.8) | copy-start | bytes 6148
